TPU v7x, 32 devices: a whole 2x2x4 slice. The times are simulated.
32 devices in a mesh: role: 2 (over x), grp: 8 (over z, y), tp: 2 (over core).
Axes of the slice: x: 2, y: 2, z: 4, core: 2. Of those that a mesh axis runs over, the one named last changes fastest.
Arguments:
- q_new: bfloat16 [256, 4096], P('grp', ('role', 'tp')), may hold values from -9 to 9
- k_new: bfloat16 [256, 512], P('grp', ('role', 'tp')), may hold values from -6 to 6
- v_new: bfloat16 [256, 512], P('grp', ('role', 'tp')), may hold values from -6 to 6
- k_cache: bfloat16 [256, 128, 512], P('grp', None, ('role', 'tp')), may hold values from -9 to 9
- v_cache: bfloat16 [256, 128, 512], P('grp', None, ('role', 'tp')), may hold values from -6 to 6
- cache_len: int32 [256], P('grp'), may hold values from 1 to 127
- cycle_start: int32 [256], P('grp'), may hold values from 0 to 127
- residual: bfloat16 [256, 2880], P('grp', ('role', 'tp')), may hold values from -6 to 6
- out_proj: bfloat16 [4096, 2880], P(('role', 'tp')), may hold values from -0.09375 to 0.09375
- norm_gain: float32 [2880], replicated, may hold values from 0.25 to 1.75
- router: bfloat16 [2880, 8], P(('role', 'tp')), may hold values from -0.21875 to 0.21875
- route_ids: int32 [256, 4], P('grp'), may hold values from 0 to 7, all different within a row; in each aligned block of 32 rows (0 to 31, 32 to 63, ...) at most 18 rows name the same one
- w_gate: bfloat16 [8, 2880, 1440], P('grp', None, ('role', 'tp')), may hold values from -0.109375 to 0.109375
- w_up: bfloat16 [8, 2880, 1440], P('grp', None, ('role', 'tp')), may hold values from -0.109375 to 0.109375
- w_down: bfloat16 [8, 1440, 2880], P('grp', ('role', 'tp')), may hold values from -0.15625 to 0.15625
Outputs:
- attended: bfloat16 [256, 2880], P('grp', ('role', 'tp'))
- expert_mix: bfloat16 [256, 2880], P('grp', ('role', 'tp'))
Inputs may be any that keep to these rules, and one draw needn't show every extreme that they name: `route_ids`: the 4 experts of a token differ. Among the tokens of one grp index (aligned blocks of 32 tokens) no expert is named more than 18 times, a bound that some block reaches.
All inputs are finite; a program needn't handle non-finite values.
Results may differ from a plain program's by a relative error of at most 0.017.
Values may be sent and summed in bfloat16 or wider, within the bound.
No kernel may reach another device: no remote copies, remote signals or barrier semaphores. Data moves between devices by JAX's collectives and lax.ppermute only.
A program may use at most 64 MiB of HBM per device.

v0:
```python
import jax
import jax.numpy as jnp
from jax import lax
from jax.sharding import PartitionSpec as P

HEADS = 64
KV_HEADS = 8
HD = 64
epsilon = 1e-05


def attend(q_new, k_new, v_new, k_cache, v_cache, cache_len, cycle_start):
    tokens = q_new.shape[0]
    window = k_cache.shape[1]
    kv_local = k_new.shape[1] // HD
    grouped = HEADS // KV_HEADS
    queries = q_new.reshape(tokens, kv_local, grouped, HD)
    cached_keys = k_cache.reshape(tokens, window, kv_local, HD)
    cached_values = v_cache.reshape(tokens, window, kv_local, HD)
    own_key = k_new.reshape(tokens, kv_local, HD)
    own_value = v_new.reshape(tokens, kv_local, HD)
    factor = HD ** (-0.5)
    scores = (
        jnp.einsum("tkgd,tskd->tkgs", queries, cached_keys, preferred_element_type=jnp.float32)
        * factor
    )
    own_score = (
        jnp.einsum("tkgd,tkd->tkg", queries, own_key, preferred_element_type=jnp.float32) * factor
    )
    positions = jnp.arange(window, dtype=jnp.int32)
    usable = (positions[None, :] - cycle_start[:, None]) % window < cache_len[:, None]
    usable = usable[:, None, None, :]
    masked = jnp.where(usable, scores, -1e30)
    highest = jnp.maximum(jnp.max(masked, axis=3), own_score)
    lifted = jnp.where(usable, jnp.exp(masked - highest[..., None]), 0.0)
    own_lift = jnp.exp(own_score - highest)
    denominator = jnp.sum(lifted, axis=3) + own_lift
    weights = (lifted / denominator[..., None]).astype(jnp.bfloat16)
    own_weight = (own_lift / denominator).astype(jnp.bfloat16)
    combined = jnp.einsum(
        "tkgs,tskd->tkgd", weights, cached_values, preferred_element_type=jnp.float32
    )
    combined = (
        combined
        + own_weight.astype(jnp.float32)[..., None] * own_value.astype(jnp.float32)[:, :, None, :]
    )
    return combined.reshape(tokens, -1).astype(jnp.bfloat16)


def slot_tables(route_ids, logits, capacity):
    experts_count = logits.shape[1]
    named = route_ids[:, :, None] == jnp.arange(experts_count, dtype=jnp.int32)
    chosen = jnp.sum(jnp.where(named, logits[:, None, :], 0.0), axis=2)
    lifted = jnp.exp(chosen)
    route_weight = lifted / jnp.sum(lifted, axis=1, keepdims=True)
    counts = jnp.sum(named.astype(jnp.int32), axis=1)
    earlier = jnp.cumsum(counts, axis=0) - counts
    ranks = jnp.sum(jnp.where(named, earlier[:, None, :], 0), axis=2)
    placed = named[:, :, :, None] & (
        ranks[:, :, None, None] == jnp.arange(capacity, dtype=jnp.int32)
    )
    select = jnp.sum(placed.astype(jnp.float32), axis=1).reshape(route_ids.shape[0], -1)
    mixing = jnp.sum(jnp.where(placed, route_weight[:, :, None, None], 0.0), axis=1).reshape(
        route_ids.shape[0], -1
    )
    return (select, mixing)


def serve(received, w_gate, w_up, w_down):
    sources = received.shape[0]
    items = received.shape[1]
    inputs = received.reshape(sources * items, received.shape[2])
    gate_lin = jnp.dot(inputs, w_gate[0], preferred_element_type=jnp.float32)
    up_lin = jnp.dot(inputs, w_up[0], preferred_element_type=jnp.float32)
    activated = (gate_lin * jax.nn.sigmoid(1.702 * gate_lin) * (up_lin + 1.0)).astype(jnp.bfloat16)
    partial_out = jnp.dot(activated, w_down[0], preferred_element_type=jnp.float32).reshape(
        sources, items, -1
    )
    rounded = lax.optimization_barrier(partial_out.astype(jnp.bfloat16))
    return lax.all_to_all(rounded, "grp", split_axis=0, concat_axis=0, tiled=True)


def local(
    q_new,
    k_new,
    v_new,
    k_cache,
    v_cache,
    cache_len,
    cycle_start,
    residual,
    out_proj,
    norm_gain,
    router,
    route_ids,
    w_gate,
    w_up,
    w_down,
):
    share = lax.axis_index(("role", "tp"))
    quarter = residual.shape[1]
    heads_out = attend(q_new, k_new, v_new, k_cache, v_cache, cache_len, cycle_start)
    projected = jnp.dot(heads_out, out_proj, preferred_element_type=jnp.float32)
    stream = lax.all_gather(residual, ("role", "tp"), axis=1, tiled=True).astype(
        jnp.float32
    ) + lax.psum(projected.astype(jnp.bfloat16), ("role", "tp")).astype(jnp.float32)
    scale = lax.rsqrt(jnp.mean(stream * stream, axis=1, keepdims=True) + epsilon)
    outgoing = (stream * scale * norm_gain).astype(jnp.bfloat16)
    own_normed = lax.dynamic_slice_in_dim(outgoing, share * quarter, quarter, 1)
    attended = lax.dynamic_slice_in_dim(stream, share * quarter, quarter, 1)
    logits = lax.psum(
        jnp.dot(own_normed, router, preferred_element_type=jnp.float32), ("role", "tp")
    )
    tokens = route_ids.shape[0]
    experts_count = logits.shape[1]
    capacity = max(3, tokens * route_ids.shape[1] // experts_count + 2)
    select, mixing = slot_tables(route_ids, logits, capacity)
    outbound = jnp.einsum(
        "ts,tf->sf", select.astype(jnp.bfloat16), outgoing, preferred_element_type=jnp.float32
    )
    outbound = outbound.astype(jnp.bfloat16).reshape(experts_count, capacity, -1)
    returned = serve(
        lax.all_to_all(outbound, "grp", split_axis=0, concat_axis=0, tiled=True),
        w_gate,
        w_up,
        w_down,
    )
    stacked = returned.reshape(-1, returned.shape[2]).astype(jnp.float32)
    combined = jnp.dot(mixing, stacked, precision=lax.Precision.HIGHEST)
    combined = lax.psum_scatter(
        combined.astype(jnp.bfloat16), ("role", "tp"), scatter_dimension=1, tiled=True
    ).astype(jnp.float32)
    return (attended.astype(jnp.bfloat16), combined.astype(jnp.bfloat16))


def solution(mesh):
    placed = (
        P("grp", ("role", "tp")),
        P("grp", ("role", "tp")),
        P("grp", ("role", "tp")),
        P("grp", None, ("role", "tp")),
        P("grp", None, ("role", "tp")),
        P("grp"),
        P("grp"),
        P("grp", ("role", "tp")),
        P(("role", "tp"), None),
        P(),
        P(("role", "tp"), None),
        P("grp", None),
        P("grp", None, ("role", "tp")),
        P("grp", None, ("role", "tp")),
        P("grp", ("role", "tp"), None),
    )
    return jax.shard_map(
        local,
        mesh=mesh,
        in_specs=placed,
        out_specs=(P("grp", ("role", "tp")), P("grp", ("role", "tp"))),
        check_vma=False,
    )
```

profile of v0, /device:TPU:0, one launch (start us, length us, event | category | flops | bytes accessed | tf_op | source)
XLA Modules:
  0.0 172.5 jit_solution(14774596593833444122)
XLA Ops:
  7.2 0.9 reshape.146
  8.2 0.8 reshape.137
  8.9 1.0 reshape.131
  10.0 0.2 fusion.38
  10.2 0.4 copy-done.2
  10.6 0.1 copy.65
  10.7 1.6 copy.52
  12.3 0.1 fusion.28
  12.4 1.4 fusion.37
  13.8 0.1 copy.53
  13.9 0.1 copy.54
  14.0 0.3 fusion.19
  14.3 0.1 copy.55
  14.3 0.1 copy.56
  14.4 0.7 copy.58
  15.1 1.6 copy.57
  16.8 2.1 %fusion.13 = bf16[32,2,8,64]{3,2,1,0:T(8,128)(2,1)} fusion(bf16[32,128,2,64]{1,3,2,0:T(8,128)(2,1)S(1)} %bitcast.66, f32[32,2,8,128]{3,2,1,0:T(8,128)S(1)} %get-tuple-element.9, f32[32,2,64]{2,1,0:T(2,128)S(1)} %reshape.137, f32[32,2,8]{2,1,0:T(2,128)} %copy.58, f32[32,2,8]{2,1,0:T(2,128)S(1)} %copy.56, f32[32,2,8]{2,1,0:T(2,128)S(1)} %copy.54, ...), kind=kOutput, calls=%fused_computation.15 | convolution fusion | flops 8749056 | bytes 1402880 | tf_op jit(solution)/shard_map/tkgs,tskd->tkgd/dot_general | solution.py:40
  18.9 1.0 convert_element_type.74
  20.0 5.2 %convolution_convert_fusion.2 = bf16[32,2880]{1,0:T(8,128)(2,1)} fusion(bf16[32,1024]{1,0:T(8,128)(2,1)S(1)} %convert_element_type.74, bf16[1024,2880]{0,1:T(8,128)(2,1)} %param.23), kind=kOutput, calls=%fused_computation.4 | convolution fusion | flops 188835840 | bytes 6148096 | tf_op jit(solution)/shard_map/dot_general | solution.py:103
  25.2 0.0 reduce-scatter.4.cloned.1.call-start
  25.3 0.1 copy.59
  25.4 0.1 reduce_window_sum.11
  25.4 0.1 copy.61
  25.6 6.9 %all-gather = bf16[4,720,32]{1,2,0:T(8,128)(2,1)S(1)} all-gather(bf16[1,720,32]{1,2,0:T(8,128)(2,1)S(1)} %bitcast.68), channel_id=1, replica_groups=mesh['role'=2,'grp'=8,'tp'=2] {'role','tp'}, dimensions={0}, use_global_device_ids=true | all-gather | bytes 230400 | tf_op jit(solution)/shard_map/all_gather | solution.py:104
  32.4 0.2 copy.51
  32.6 0.2 reshape.140
  32.9 27.2 %all-reduce.2.cloned.1.call-done = bf16[32,2880]{1,0:T(8,128)(2,1)} async-done(((bf16[32,2880]{1,0:T(8,128)(2,1)}), bf16[32,2880]{1,0:T(8,128)(2,1)}) %all-reduce.2.cloned.1.call-update) | async-done | bytes 184336 | tf_op jit(solution)/shard_map/psum | solution.py:106
  60.0 1.1 multiply_reduce_fusion
  61.1 0.7 copy-done.1
  61.9 0.1 multiply_convert_fusion
  62.0 0.2 fusion.25
  62.2 5.7 %psum.15 = f32[32,8]{0,1:T(8,128)S(1)} all-reduce(f32[32,8]{0,1:T(8,128)S(1)} %fusion.25), channel_id=1, replica_groups=mesh['role'=2,'grp'=8,'tp'=2] {'role','tp'}, use_global_device_ids=true, to_apply=%region_7.8 | all-reduce | flops 256 | bytes 2048 | tf_op jit(solution)/shard_map/psum | solution.py:111
  68.0 0.1 fusion.17
  68.1 0.2 copy.62
  68.2 0.1 convert_element_type.82
  68.4 1.3 convolution_convert_fusion.1
  69.7 1.4 reshape.135
  71.1 33.4 %all_to_all.10 = bf16[8,18,2880]{2,1,0:T(8,128)(2,1)} all-to-all(bf16[8,18,2880]{2,1,0:T(8,128)(2,1)S(1)} %reshape.135), channel_id=1, replica_groups=mesh['role'=2,'grp'=8,'tp'=2] {'grp'}, dimensions={0} | all-to-all | bytes 1658880 | tf_op jit(solution)/shard_map/all_to_all | solution.py:123
  104.6 1.7 reshape.136
  106.3 2.6 %fusion.4 = f32[144,360]{1,0:T(8,128)S(1)} fusion(bf16[144,2880]{1,0:T(8,128)(2,1)S(1)} %reshape.136, bf16[1,2880,360]{1,2,0:T(8,128)(2,1)} %param.27), kind=kOutput, calls=%fused_computation.8 | convolution fusion | flops 298598400 | bytes 3110400 | tf_op jit(solution)/shard_map/dot_general | solution.py:73
  108.9 0.8 fusion.14
  109.8 0.8 convolution_convert_fusion
  110.6 30.5 %all_to_all.11 = bf16[8,18,2880]{2,1,0:T(8,128)(2,1)S(1)} all-to-all(bf16[8,18,2880]{2,1,0:T(8,128)(2,1)S(1)} %convolution_convert_fusion), channel_id=1, replica_groups=mesh['role'=2,'grp'=8,'tp'=2] {'grp'}, dimensions={0} | all-to-all | bytes 1658880 | tf_op jit(solution)/shard_map/all_to_all | solution.py:80
  141.1 0.8 fusion
  141.9 1.2 copy.66
  143.1 1.6 dynamic-slice_convert_fusion
  144.7 19.3 %reduce-scatter.4.cloned.1.call-done = bf16[720,32]{1,0:T(8,128)(2,1)} async-done(((bf16[2880,32]{1,0:T(8,128)(2,1)}), bf16[720,32]{1,0:T(8,128)(2,1)}) %reduce-scatter.4.cloned.1.call-update) | async-done | bytes 46096
  164.0 1.7 copy.67
  (33 shorter events, 0.3 us)
Async XLA Ops:
  7.2 102.6 %copy-start = (bf16[1,360,2880]{2,1,0:T(8,128)(2,1)S(1)}, bf16[1,360,2880]{2,1,0:T(8,128)(2,1)}, u32[]{:S(2)}) copy-start(bf16[1,360,2880]{2,1,0:T(8,128)(2,1)} %param.29) | copy-start | bytes 6220804
  7.2 5.1 %copy-start.8 = (s32[32]{0:T(128)S(1)}, s32[32]{0:T(128)}, u32[]{:S(2)}) copy-start(s32[32]{0:T(128)} %param.21) | copy-start | bytes 388
  7.2 5.1 %copy-start.7 = (s32[32]{0:T(128)S(1)}, s32[32]{0:T(128)}, u32[]{:S(2)}) copy-start(s32[32]{0:T(128)} %param.20) | copy-start | bytes 388
  7.2 52.8 %all-reduce.2.cloned.1.call-start = ((), (), s32[]{:S(2)}) async-start(), calls=%async_computation.3 | async-start | bytes 376832 | tf_op jit(solution)/shard_map/psum | solution.py:106
  10.0 0.6 copy-start.2
  19.9 5.3 %copy-start.4 = (s32[32,4]{0,1:T(4,128)S(1)}, s32[32,4]{0,1:T(4,128)}, u32[]{:S(2)}) copy-start(s32[32,4]{0,1:T(4,128)} %param.26) | copy-start | bytes 1540
  20.0 5.6 %copy-start.3 = (bf16[32,720]{1,0:T(8,128)(2,1)S(1)}, bf16[32,720]{1,0:T(8,128)(2,1)}, u32[]{:S(2)}) copy-start(bf16[32,720]{1,0:T(8,128)(2,1)} %param.22) | copy-start | bytes 138244
  25.2 36.7 %copy-start.6 = (f32[2880]{0:T(1024)S(1)}, f32[2880]{0:T(1024)}, u32[]{:S(2)}) copy-start(f32[2880]{0:T(1024)} %param.24) | copy-start | bytes 34564
  25.2 36.8 %copy-start.5 = (bf16[720,8]{0,1:T(8,128)(2,1)S(1)}, bf16[720,8]{0,1:T(8,128)(2,1)}, u32[]{:S(2)}) copy-start(bf16[720,8]{0,1:T(8,128)(2,1)} %param.25) | copy-start | bytes 34564
  25.2 138.8 %reduce-scatter.4.cloned.1.call-start = ((), (), s32[]{:S(2)}) async-start(), calls=%async_computation.4 | async-start | bytes 921600
  61.1 0.8 copy-start.1
  106.3 2.6 %copy-start.9 = (bf16[1,2880,360]{1,2,0:T(8,128)(2,1)S(1)}, bf16[1,2880,360]{1,2,0:T(8,128)(2,1)}, u32[]{:S(2)}) copy-start(bf16[1,2880,360]{1,2,0:T(8,128)(2,1)} %param.28) | copy-start | bytes 6220804
Sparse Core Ops, SparseCore 0:
  25.3 34.6 all-reduce.1
  143.2 20.7 reduce-scatter.3
where the time goes:
time: 173 us
  blocking collectives  76.6 us (44%)
  waiting for transfers between devices  46.5 us (27%)
  local copies, waits for them, and re-layouts  17.7 us (10%)
  matrix products  15.4 us (9%)
  between operations  14.3 us (8%)
  other arithmetic  1.84 us (1%)
    all_to_all x1, blocking collectives, local(): lax.all_to_all(outbound, 'grp', split_axis=0, concat_axis=0, tiled=True)  33.4 us
    all_to_all x1, blocking collectives, serve(): lax.all_to_all(rounded, 'grp', split_axis=0, concat_axis=0, tiled=True)  30.5 us
    psum x1, waiting for transfers between devices, local(): lax.psum(projected.astype(jnp.bfloat16), ('role', 'tp')).astype(jnp.float32)  27.2 us
    unnamed x3, waiting for transfers between devices  19.3 us
    unnamed x24, local copies, waits for them, and re-layouts  7.26 us
    all_gather x1, blocking collectives, local(): lax.all_gather(residual, ('role', 'tp'), axis=1, tiled=True)  6.87 us
    psum x1, blocking collectives, local(): lax.psum(jnp.dot(own_normed, router, preferred_element_type=jnp.float32),...  5.74 us
    dot_general x1, matrix products, local(): projected = jnp.dot(heads_out, out_proj, preferred_element_type=jnp.float32)  5.22 us
  transfers between devices with their start and end apart: 2, of which 2 were waited for; matrix products, arithmetic and copies ran while one was open for 1% of the time, Pallas kernels for 0%

commit v1 on v0

--- a/solution.py
+++ b/solution.py
@@ -103,7 +103,7 @@
     projected = jnp.dot(heads_out, out_proj, preferred_element_type=jnp.float32)
     stream = lax.all_gather(residual, ("role", "tp"), axis=1, tiled=True).astype(
         jnp.float32
-    ) + lax.psum(projected.astype(jnp.bfloat16), ("role", "tp")).astype(jnp.float32)
+    ) + lax.psum(lax.psum(projected.astype(jnp.bfloat16), "tp"), "role").astype(jnp.float32)
     scale = lax.rsqrt(jnp.mean(stream * stream, axis=1, keepdims=True) + epsilon)
     outgoing = (stream * scale * norm_gain).astype(jnp.bfloat16)
     own_normed = lax.dynamic_slice_in_dim(outgoing, share * quarter, quarter, 1)

time: 173 us -> 185 us (1.069)
  waiting for transfers between devices: 46.5 us -> 58.1 us
    psum x1 -> x2, waiting for transfers between devices: 27.2 us -> 39.1 us  [the longest x1 25.8 us: local(): lax.psum(lax.psum(projected.astype(jnp.bfloat16), 'tp'), 'role')]
    unnamed x3 -> x4, waiting for transfers between devices: 19.3 us -> 19 us
  transfers between devices with their start and end apart: 2 -> 3, of which waited for: 2 -> 3; matrix products, arithmetic and copies ran while one was open for 1% -> 1% of each run, Pallas kernels for 0% -> 0%
where the time goes in v1:
time: 185 us; the launch traced here: 184 us
  blocking collectives  76.9 us (42%)
  waiting for transfers between devices  58.1 us (31%)
  local copies, waits for them, and re-layouts  17.7 us (10%)
  matrix products  15.5 us (8%)
  between operations  14 us (8%)
    all_to_all x1, blocking collectives, local(): lax.all_to_all(outbound, 'grp', split_axis=0, concat_axis=0, tiled=True)  33.4 us
    all_to_all x1, blocking collectives, serve(): lax.all_to_all(rounded, 'grp', split_axis=0, concat_axis=0, tiled=True)  30.8 us
    psum x1, waiting for transfers between devices, local(): lax.psum(lax.psum(projected.astype(jnp.bfloat16), 'tp'), 'role')  25.8 us
    unnamed x4, waiting for transfers between devices  19 us
    psum x1, waiting for transfers between devices, local(): lax.psum(projected.astype(jnp.bfloat16), 'tp')  13.3 us
    unnamed x24, local copies, waits for them, and re-layouts  7.26 us
    all_gather x1, blocking collectives, local(): lax.all_gather(residual, ('role', 'tp'), axis=1, tiled=True)  6.87 us
    psum x1, blocking collectives, local(): lax.psum(jnp.dot(own_normed, router, preferred_element_type=jnp.float32),...  5.74 us
  transfers between devices with their start and end apart: 3, of which 3 were waited for; matrix products, arithmetic and copies ran while one was open for 1% of the time, Pallas kernels for 0%

profile of v1, /device:TPU:0, one launch (start us, length us, event | category | flops | bytes accessed | tf_op | source)
XLA Modules:
  0.0 184.1 jit_solution(5130874727245528129)
XLA Ops:
  7.2 0.9 reshape.146
  8.2 0.8 reshape.137
  8.9 1.0 reshape.131
  10.0 0.2 fusion.38
  10.2 0.4 copy-done.2
  10.6 0.1 copy.65
  10.7 1.6 copy.52
  12.3 0.1 fusion.28
  12.4 1.4 fusion.37
  13.8 0.1 copy.53
  13.9 0.1 copy.54
  14.0 0.3 fusion.19
  14.3 0.1 copy.55
  14.3 0.1 copy.56
  14.4 0.7 copy.58
  15.1 1.6 copy.57
  16.8 2.1 %fusion.13 = bf16[32,2,8,64]{3,2,1,0:T(8,128)(2,1)} fusion(bf16[32,128,2,64]{1,3,2,0:T(8,128)(2,1)S(1)} %bitcast.66, f32[32,2,8,128]{3,2,1,0:T(8,128)S(1)} %get-tuple-element.9, f32[32,2,64]{2,1,0:T(2,128)S(1)} %reshape.137, f32[32,2,8]{2,1,0:T(2,128)} %copy.58, f32[32,2,8]{2,1,0:T(2,128)S(1)} %copy.56, f32[32,2,8]{2,1,0:T(2,128)S(1)} %copy.54, ...), kind=kOutput, calls=%fused_computation.15 | convolution fusion | flops 8749056 | bytes 1402880 | tf_op jit(solution)/shard_map/tkgs,tskd->tkgd/dot_general | solution.py:40
  18.9 1.0 convert_element_type.74
  20.0 5.2 %convolution_convert_fusion.2 = bf16[32,2880]{1,0:T(8,128)(2,1)} fusion(bf16[32,1024]{1,0:T(8,128)(2,1)S(1)} %convert_element_type.74, bf16[1024,2880]{0,1:T(8,128)(2,1)} %param.23), kind=kOutput, calls=%fused_computation.4 | convolution fusion | flops 188835840 | bytes 6148096 | tf_op jit(solution)/shard_map/dot_general | solution.py:103
  25.3 0.1 copy.59
  25.4 0.1 reduce_window_sum.11
  25.4 0.1 copy.61
  25.5 6.9 %all-gather = bf16[4,720,32]{1,2,0:T(8,128)(2,1)S(1)} all-gather(bf16[1,720,32]{1,2,0:T(8,128)(2,1)S(1)} %bitcast.68), channel_id=1, replica_groups=mesh['role'=2,'grp'=8,'tp'=2] {'role','tp'}, dimensions={0}, use_global_device_ids=true | all-gather | bytes 230400 | tf_op jit(solution)/shard_map/all_gather | solution.py:104
  32.4 0.2 copy.51
  32.6 0.2 reshape.140
  32.8 13.3 %all-reduce.3.cloned.1.call-done = bf16[32,2880]{1,0:T(8,128)(2,1)} async-done(((bf16[32,2880]{1,0:T(8,128)(2,1)}), bf16[32,2880]{1,0:T(8,128)(2,1)}) %all-reduce.3.cloned.1.call-update) | async-done | bytes 184336 | tf_op jit(solution)/shard_map/psum | solution.py:106
  46.2 25.8 %all-reduce.5.cloned.1.call-done = bf16[32,2880]{1,0:T(8,128)(2,1)} async-done(((bf16[32,2880]{1,0:T(8,128)(2,1)}), bf16[32,2880]{1,0:T(8,128)(2,1)}) %all-reduce.5.cloned.1.call-update) | async-done | bytes 184336 | tf_op jit(solution)/shard_map/psum | solution.py:106
  72.0 1.1 multiply_reduce_fusion
  73.1 0.7 copy-done.1
  73.8 0.1 multiply_convert_fusion
  74.0 0.2 fusion.25
  74.2 5.7 %psum.23 = f32[32,8]{0,1:T(8,128)S(1)} all-reduce(f32[32,8]{0,1:T(8,128)S(1)} %fusion.25), channel_id=1, replica_groups=mesh['role'=2,'grp'=8,'tp'=2] {'role','tp'}, use_global_device_ids=true, to_apply=%region_8.9 | all-reduce | flops 256 | bytes 2048 | tf_op jit(solution)/shard_map/psum | solution.py:111
  80.0 0.1 fusion.17
  80.1 0.2 copy.62
  80.2 0.1 convert_element_type.82
  80.3 1.3 convolution_convert_fusion.1
  81.6 1.4 reshape.135
  83.1 33.4 %all_to_all.10 = bf16[8,18,2880]{2,1,0:T(8,128)(2,1)} all-to-all(bf16[8,18,2880]{2,1,0:T(8,128)(2,1)S(1)} %reshape.135), channel_id=1, replica_groups=mesh['role'=2,'grp'=8,'tp'=2] {'grp'}, dimensions={0} | all-to-all | bytes 1658880 | tf_op jit(solution)/shard_map/all_to_all | solution.py:123
  116.5 1.7 reshape.136
  118.3 2.6 %fusion.4 = f32[144,360]{1,0:T(8,128)S(1)} fusion(bf16[144,2880]{1,0:T(8,128)(2,1)S(1)} %reshape.136, bf16[1,2880,360]{1,2,0:T(8,128)(2,1)} %param.27), kind=kOutput, calls=%fused_computation.8 | convolution fusion | flops 298598400 | bytes 3110400 | tf_op jit(solution)/shard_map/dot_general | solution.py:73
  120.8 0.8 fusion.14
  121.7 0.8 convolution_convert_fusion
  122.5 30.8 %all_to_all.11 = bf16[8,18,2880]{2,1,0:T(8,128)(2,1)S(1)} all-to-all(bf16[8,18,2880]{2,1,0:T(8,128)(2,1)S(1)} %convolution_convert_fusion), channel_id=1, replica_groups=mesh['role'=2,'grp'=8,'tp'=2] {'grp'}, dimensions={0} | all-to-all | bytes 1658880 | tf_op jit(solution)/shard_map/all_to_all | solution.py:80
  153.3 0.8 fusion
  154.1 1.2 copy.66
  155.3 1.6 dynamic-slice_convert_fusion
  156.9 19.0 %reduce-scatter.4.cloned.1.call-done = bf16[720,32]{1,0:T(8,128)(2,1)} async-done(((bf16[2880,32]{1,0:T(8,128)(2,1)}), bf16[720,32]{1,0:T(8,128)(2,1)}) %reduce-scatter.4.cloned.1.call-update) | async-done | bytes 46096
  175.9 1.7 copy.67
  (36 shorter events, 0.4 us)
Async XLA Ops:
  7.2 114.6 %copy-start = (bf16[1,360,2880]{2,1,0:T(8,128)(2,1)S(1)}, bf16[1,360,2880]{2,1,0:T(8,128)(2,1)}, u32[]{:S(2)}) copy-start(bf16[1,360,2880]{2,1,0:T(8,128)(2,1)} %param.29) | copy-start | bytes 6220804
  7.2 5.1 %copy-start.8 = (s32[32]{0:T(128)S(1)}, s32[32]{0:T(128)}, u32[]{:S(2)}) copy-start(s32[32]{0:T(128)} %param.21) | copy-start | bytes 388
  7.2 5.1 %copy-start.7 = (s32[32]{0:T(128)S(1)}, s32[32]{0:T(128)}, u32[]{:S(2)}) copy-start(s32[32]{0:T(128)} %param.20) | copy-start | bytes 388
  7.2 38.9 %all-reduce.3.cloned.1.call-start = ((), (), s32[]{:S(2)}) async-start(), calls=%async_computation.3 | async-start | bytes 376832 | tf_op jit(solution)/shard_map/psum | solution.py:106
  10.0 0.6 copy-start.2
  19.9 5.3 %copy-start.4 = (s32[32,4]{0,1:T(4,128)S(1)}, s32[32,4]{0,1:T(4,128)}, u32[]{:S(2)}) copy-start(s32[32,4]{0,1:T(4,128)} %param.26) | copy-start | bytes 1540
  20.0 5.6 %copy-start.3 = (bf16[32,720]{1,0:T(8,128)(2,1)S(1)}, bf16[32,720]{1,0:T(8,128)(2,1)}, u32[]{:S(2)}) copy-start(bf16[32,720]{1,0:T(8,128)(2,1)} %param.22) | copy-start | bytes 138244
  25.2 48.6 %copy-start.6 = (f32[2880]{0:T(1024)S(1)}, f32[2880]{0:T(1024)}, u32[]{:S(2)}) copy-start(f32[2880]{0:T(1024)} %param.24) | copy-start | bytes 34564
  25.2 48.8 %copy-start.5 = (bf16[720,8]{0,1:T(8,128)(2,1)S(1)}, bf16[720,8]{0,1:T(8,128)(2,1)}, u32[]{:S(2)}) copy-start(bf16[720,8]{0,1:T(8,128)(2,1)} %param.25) | copy-start | bytes 34564
  25.2 46.8 %all-reduce.5.cloned.1.call-start = ((), (), s32[]{:S(2)}) async-start(), calls=%async_computation.4 | async-start | bytes 376832 | tf_op jit(solution)/shard_map/psum | solution.py:106
  46.2 129.8 %reduce-scatter.4.cloned.1.call-start = ((), (), s32[]{:S(2)}) async-start(), calls=%async_computation.5 | async-start | bytes 921600
  73.1 0.8 copy-start.1
  118.2 2.6 %copy-start.9 = (bf16[1,2880,360]{1,2,0:T(8,128)(2,1)S(1)}, bf16[1,2880,360]{1,2,0:T(8,128)(2,1)}, u32[]{:S(2)}) copy-start(bf16[1,2880,360]{1,2,0:T(8,128)(2,1)} %param.28) | copy-start | bytes 6220804
Sparse Core Ops, SparseCore 0:
  25.3 20.7 all-reduce.2
  48.4 23.5 all-reduce.4
  155.4 20.4 reduce-scatter.3
